TPU v7x, 32 devices: a whole 2x2x4 slice. The times are simulated.
32 devices in a mesh: tp: 8 (over z, y), dp: 4 (over x, core).
Axes of the slice: x: 2, y: 2, z: 4, core: 2. Of those that a mesh axis runs over, the one named last changes fastest.
Arguments:
- tokens: bfloat16 [32, 8192], P(None, ('dp', 'tp')), may hold values from -6 to 6
- query_weight: bfloat16 [8192, 8192], P('dp', 'tp'), may hold values from -0.0625 to 0.0625
- key_weight: bfloat16 [8192, 1024], P('dp', 'tp'), may hold values from -0.0625 to 0.0625
- value_weight: bfloat16 [8192, 1024], P('dp', 'tp'), may hold values from -0.0625 to 0.0625
- query_bias: bfloat16 [8192], P('tp'), may hold values from -3 to 3
- key_bias: bfloat16 [1024], P('tp'), may hold values from -6 to 6
- value_bias: bfloat16 [1024], P('tp'), may hold values from -6 to 6
- out_weight: bfloat16 [8192, 8192], P('tp', 'dp'), may hold values from -0.0625 to 0.0625
- key_pool: bfloat16 [2048, 16, 8, 128], P(('dp', 'tp')), may hold values from -12 to 12
- value_pool: bfloat16 [2048, 16, 8, 128], P(('dp', 'tp')), may hold values from -9 to 9
- page_table: int32 [32, 64], P('dp'), may hold values from 0 to 2047, as said below
- lengths: int32 [32], P('dp'), may hold values from 512 to 1023
Outputs:
- mixed: bfloat16 [32, 8192], P(None, ('dp', 'tp'))
- key_out: bfloat16 [2048, 16, 8, 128], P(('dp', 'tp'))
- value_out: bfloat16 [2048, 16, 8, 128], P(('dp', 'tp'))
Inputs may be any that keep to these rules, and one draw needn't show every extreme that they name: page_table[b, j] is the pool page that holds positions 16 j to 16 j + 16 - 1 of sequence b; every page of the pool is named exactly once; page_table[b, j] // 64 equals (b // 8) * 8 + j % 8, so that page lies on the device of dp index b // 8 and tp index j % 8. lengths[b] is the position of sequence b's new token; positions 0 to lengths[b] - 1 of the cache hold earlier tokens.
All inputs are finite; a program needn't handle non-finite values.
Results may differ from a plain program's by a relative error of at most 0.007.
Values may be sent and summed in bfloat16 or wider, within the bound.
A program may use at most 64 MiB of HBM per device.

v0:
```python
import jax
import jax.numpy as jnp
from jax import lax
from jax.sharding import PartitionSpec as P

rope_theta = 1000000.0
mask_value = -1e30


def summed_rows(portion, rows, axis):
    count = rows * lax.axis_size(axis)
    return lax.psum_scatter(portion(jnp.int32(0), count), axis, scatter_dimension=0, tiled=True)


def rotate(vectors, position):
    head_width = vectors.shape[-1]
    half_width = head_width // 2
    frequency = rope_theta ** (-(jnp.arange(half_width, dtype=jnp.float32) * 2.0 / head_width))
    angles = position.astype(jnp.float32)[:, None] * frequency[None, :]
    cosine = jnp.cos(angles)[:, None, :]
    sine_part = jnp.sin(angles)[:, None, :]
    leading = vectors[..., :half_width]
    trailing = vectors[..., half_width:]
    return jnp.concatenate(
        [leading * cosine - trailing * sine_part, trailing * cosine + leading * sine_part], axis=-1
    )


def local(
    tokens,
    query_weight,
    key_weight,
    value_weight,
    query_bias,
    key_bias,
    value_bias,
    out_weight,
    key_pool,
    value_pool,
    page_table,
    lengths,
):
    tp_width = lax.axis_size("tp")
    tp_place = lax.axis_index("tp")
    seq_rows = page_table.shape[0]
    slot_count, page_rows, kv_heads, head_width = key_pool.shape
    query_cols = query_weight.shape[1]
    key_cols = key_weight.shape[1]
    local_heads = query_cols // head_width
    head_count = local_heads * tp_width
    group_size = head_count // kv_heads
    local_pages = page_table.shape[1] // tp_width
    columns = lax.all_gather(tokens, "tp", axis=1, tiled=True)

    def project(first_row, row_count):
        row_block = lax.dynamic_slice_in_dim(columns, first_row, row_count, 0)
        return jnp.concatenate(
            [
                jnp.dot(row_block, query_weight, preferred_element_type=jnp.float32),
                jnp.dot(row_block, key_weight, preferred_element_type=jnp.float32),
                jnp.dot(row_block, value_weight, preferred_element_type=jnp.float32),
            ],
            axis=1,
        )

    projected = summed_rows(project, seq_rows, "dp")
    query_lin = projected[:, :query_cols] + query_bias.astype(jnp.float32)
    key_lin = projected[:, query_cols : query_cols + key_cols] + key_bias.astype(jnp.float32)
    value_lin = projected[:, query_cols + key_cols :] + value_bias.astype(jnp.float32)
    local_query = rotate(query_lin.reshape(seq_rows, local_heads, head_width), lengths).astype(
        jnp.bfloat16
    )
    query_rows = lax.all_gather(local_query.reshape(seq_rows, query_cols), "tp", axis=1, tiled=True)
    key_full, value_full = (
        lax.all_gather(key_lin, "tp", axis=1, tiled=True),
        lax.all_gather(value_lin, "tp", axis=1, tiled=True),
    )
    new_key = rotate(key_full.reshape(seq_rows, kv_heads, head_width), lengths).astype(jnp.bfloat16)
    new_value = value_full.reshape(seq_rows, kv_heads, head_width).astype(jnp.bfloat16)
    page_index = lengths // page_rows
    offset = lengths % page_rows
    owner_here = page_index % tp_width == tp_place
    target = jnp.take_along_axis(page_table, page_index[:, None], axis=1)[:, 0] % slot_count
    target = jnp.where(owner_here, target, slot_count)
    key_out = key_pool.at[target, offset].set(new_key, mode="drop")
    value_out = value_pool.at[target, offset].set(new_value, mode="drop")
    local_ids = (
        lax.dynamic_index_in_dim(
            page_table.reshape(seq_rows, local_pages, tp_width), tp_place, 2, keepdims=False
        )
        % slot_count
    )
    page_start = (jnp.arange(local_pages, dtype=jnp.int32) * tp_width + tp_place) * page_rows
    positions = (page_start[:, None] + jnp.arange(page_rows, dtype=jnp.int32)[None, :]).reshape(-1)
    local_span = local_pages * page_rows
    score_scale = head_width ** (-0.5)

    def attend(inputs):
        head_query, slot_ids, length = inputs
        key_rows = key_out[slot_ids].reshape(local_span, kv_heads, head_width)
        value_rows = (
            value_out[slot_ids].reshape(local_span, kv_heads, head_width).astype(jnp.float32)
        )
        grouped = head_query.reshape(kv_heads, group_size, head_width)
        scores = (
            jnp.einsum("gqd,sgd->gqs", grouped, key_rows, preferred_element_type=jnp.float32)
            * score_scale
        )
        scores = jnp.where(positions[None, None, :] <= length, scores, mask_value)
        row_peak = jnp.max(scores, axis=-1)
        powered = jnp.exp(scores - row_peak[..., None])
        partial_value = jnp.einsum(
            "gqs,sgd->gqd", powered, value_rows, precision=lax.Precision.HIGHEST
        )
        return (
            partial_value.reshape(head_count, head_width),
            row_peak.reshape(head_count),
            jnp.sum(powered, axis=-1).reshape(head_count),
        )

    partial_value, row_peak, row_total = lax.map(attend, (query_rows, local_ids, lengths))
    packed = jnp.concatenate([partial_value, row_peak[..., None], row_total[..., None]], axis=-1)[
        None
    ]
    received = lax.all_to_all(packed, "tp", split_axis=2, concat_axis=0, tiled=True)
    peak_rows = received[..., head_width]
    highest = jnp.max(peak_rows, axis=0)
    factors = jnp.exp(peak_rows - highest[None])
    own_sum = jnp.sum(received[..., :head_width] * factors[..., None], axis=0)
    own_total = jnp.sum(received[..., head_width + 1] * factors, axis=0)
    attended = (own_sum / own_total[..., None]).reshape(seq_rows, query_cols).astype(jnp.bfloat16)
    batch_heads = lax.all_gather(attended, "dp", axis=0, tiled=True)

    def mix(first_row, row_count):
        weight_block = lax.dynamic_slice_in_dim(out_weight, first_row, row_count, 1)
        return lax.dot_general(
            weight_block, batch_heads, (((0,), (1,)), ((), ())), preferred_element_type=jnp.float32
        )

    out_rows = out_weight.shape[1] // tp_width
    mixed = summed_rows(mix, out_rows, "tp")
    return (mixed.T.astype(jnp.bfloat16), key_out, value_out)


def solution(mesh):
    in_specs = (
        P(None, ("dp", "tp")),
        P("dp", "tp"),
        P("dp", "tp"),
        P("dp", "tp"),
        P("tp"),
        P("tp"),
        P("tp"),
        P("tp", "dp"),
        P(("dp", "tp"), None, None, None),
        P(("dp", "tp"), None, None, None),
        P("dp", None),
        P("dp"),
    )
    out_specs = (
        P(None, ("dp", "tp")),
        P(("dp", "tp"), None, None, None),
        P(("dp", "tp"), None, None, None),
    )
    return jax.shard_map(local, mesh=mesh, in_specs=in_specs, out_specs=out_specs, check_vma=False)
```

profile of v0, /device:TPU:0, one launch (start us, length us, event | category | flops | bytes accessed | tf_op | source)
XLA Modules:
  0.0 311.2 jit_solution(8114477693743469053)
XLA Ops:
  7.3 3.3 %copy.161 = bf16[64,16,8,128]{3,2,1,0:T(8,128)(2,1)} copy(bf16[64,16,8,128]{3,2,1,0:T(8,128)(2,1)} %param.22) | data formatting | bytes 4194304
  10.6 32.5 %all_gather.15 = bf16[32,2048]{1,0:T(8,128)(2,1)S(1)} all-gather(bf16[32,256]{1,0:T(8,128)(2,1)S(1)} %copy-done.6), channel_id=1, replica_groups=mesh['tp'=8,'dp'=4] {'tp'}, dimensions={1}, use_global_device_ids=true | all-gather | bytes 147456 | tf_op jit(solution)/shard_map/all_gather | solution.py:53
  43.6 0.8 fusion.26
  46.5 19.4 %reduce-scatter.3.cloned.1.call-done = f32[8,1280]{1,0:T(8,128)} async-done(((f32[32,1280]{1,0:T(8,128)}), f32[8,1280]{1,0:T(8,128)}) %reduce-scatter.3.cloned.1.call-update) | async-done | bytes 40976 | tf_op jit(solution)/shard_map/reduce_scatter | solution.py:12
  66.5 30.5 %all_gather.18 = bf16[8,1024]{1,0:T(8,128)(2,1)S(1)} all-gather(bf16[8,128]{1,0:T(8,128)(2,1)S(1)} %slice_add_fusion.1), channel_id=1, replica_groups=mesh['tp'=8,'dp'=4] {'tp'}, dimensions={1}, use_global_device_ids=true | all-gather | bytes 18432 | tf_op jit(solution)/shard_map/all_gather | solution.py:76
  97.7 30.4 %all_gather.17 = f32[8,1024]{1,0:T(8,128)S(1)} all-gather(f32[8,128]{1,0:T(8,128)S(1)} %slice_add_fusion.2), channel_id=1, replica_groups=mesh['tp'=8,'dp'=4] {'tp'}, dimensions={1}, use_global_device_ids=true | all-gather | bytes 36864 | tf_op jit(solution)/shard_map/all_gather | solution.py:75
  129.2 30.5 %all_gather.16 = bf16[8,8192]{1,0:T(8,128)(2,1)S(1)} all-gather(bf16[8,1024]{1,0:T(8,128)(2,1)S(1)} %bitcast.109), channel_id=1, replica_groups=mesh['tp'=8,'dp'=4] {'tp'}, dimensions={1}, use_global_device_ids=true | all-gather | bytes 147456 | tf_op jit(solution)/shard_map/all_gather | solution.py:73
  159.8 2.1 scatter_fusion
  162.7 44.7 %while.15 = (s32[]{:T(128)}, f32[8,64,128]{2,0,1:T(8,128)S(1)}, f32[8,64]{1,0:T(8,128)S(1)}, f32[8,64]{1,0:T(8,128)S(1)}, s32[8]{0:T(128)S(1)}, /*index=5*/bf16[...) while((s32[]{:T(128)}, f32[8,64,128]{2,0,1:T(8,128)S(1)}, ...), condition=%wide.region_6.7_spmd.clone, body=%wide.region_3.6_spmd.clone.sunk | while | flops 14730394 | bytes 1826657 | solution.py:121
  164.2 2.2 gather_fusion.1
  169.8 2.2 gather_fusion.1
  175.4 2.2 gather_fusion.1
  181.0 2.2 gather_fusion.1
  186.6 2.2 gather_fusion.1
  192.2 2.2 gather_fusion.1
  197.8 2.2 gather_fusion.1
  203.4 2.2 gather_fusion.1
  207.9 16.0 %all_to_all.18 = f32[1,8,64,130]{3,1,0,2:T(8,128)S(1)} all-to-all(f32[1,8,64,130]{3,1,0,2:T(8,128)S(1)} %maximum_bitcast_fusion), channel_id=1, replica_groups=mesh['tp'=8,'dp'=4] {'tp'}, dimensions={2} | all-to-all | bytes 532480 | tf_op jit(solution)/shard_map/all_to_all | solution.py:125
  223.9 3.8 %copy.106 = f32[1,8,8,8,130]{3,1,4,2,0:T(8,128)} copy(f32[1,8,8,8,130]{4,1,3,2,0:T(8,128)S(1)} %bitcast.107) | data formatting | bytes 532480 | tf_op jit(solution)/shard_map/all_to_all | solution.py:125
  230.0 2.7 fusion.10
  232.9 5.2 %all_gather.19 = bf16[32,1024]{1,0:T(8,128)(2,1)S(1)} all-gather(bf16[8,1024]{1,0:T(8,128)(2,1)S(1)} %bitcast.111), channel_id=1, replica_groups=mesh['tp'=8,'dp'=4] {'dp'}, dimensions={0}, use_global_device_ids=true | all-gather | bytes 81920 | tf_op jit(solution)/shard_map/all_gather | solution.py:132
  238.2 3.7 %convolution_bitcast_fusion = f32[2048,32]{0,1:T(8,128)} fusion(bf16[32,1024]{1,0:T(8,128)(2,1)S(1)} %all_gather.19, bf16[1024,2048]{1,0:T(8,128)(2,1)} %param.21), kind=kOutput, calls=%fused_computation.22 | convolution fusion | flops 134217728 | bytes 4521984 | tf_op jit(solution)/shard_map/dot_general | solution.py:136
  241.9 61.1 %reduce-scatter.5.cloned.1.call-done = f32[256,32]{0,1:T(8,128)} async-done(((f32[2048,32]{0,1:T(8,128)}), f32[256,32]{0,1:T(8,128)}) %reduce-scatter.5.cloned.1.call-update) | async-done | bytes 32784 | tf_op jit(solution)/shard_map/reduce_scatter | solution.py:12
  303.0 1.4 convert_bitcast_fusion
  (187 shorter events, 35.5 us)
Async XLA Ops:
  7.2 36.0 %copy-start = (bf16[2048,128]{1,0:T(8,128)(2,1)S(1)}, bf16[2048,128]{1,0:T(8,128)(2,1)}, u32[]{:S(2)}) copy-start(bf16[2048,128]{1,0:T(8,128)(2,1)} %param.17) | copy-start | bytes 1572868
  7.2 3.4 %copy-start.6 = (bf16[32,256]{1,0:T(8,128)(2,1)S(1)}, bf16[32,256]{1,0:T(8,128)(2,1)}, u32[]{:S(2)}) copy-start(bf16[32,256]{1,0:T(8,128)(2,1)} %param.14) | copy-start | bytes 49156
  7.2 36.1 %copy-start.5 = (bf16[2048,128]{1,0:T(8,128)(2,1)S(1)}, bf16[2048,128]{1,0:T(8,128)(2,1)}, u32[]{:S(2)}) copy-start(bf16[2048,128]{1,0:T(8,128)(2,1)} %param.16) | copy-start | bytes 1572868
  7.2 58.7 %reduce-scatter.3.cloned.1.call-start = ((), (), s32[]{:S(2)}) async-start(), calls=%async_computation.3 | async-start | bytes 204800 | tf_op jit(solution)/shard_map/reduce_scatter | solution.py:12
  7.2 36.3 %copy-start.4 = (bf16[2048,1024]{1,0:T(8,128)(2,1)S(1)}, bf16[2048,1024]{1,0:T(8,128)(2,1)}, u32[]{:S(2)}) copy-start(bf16[2048,1024]{1,0:T(8,128)(2,1)} %param.15) | copy-start | bytes 12582916
  10.6 34.6 %copy-start.9 = (bf16[128]{0:T(256)(128)(2,1)S(1)}, bf16[128]{0:T(256)(128)(2,1)}, u32[]{:S(2)}) copy-start(bf16[128]{0:T(256)(128)(2,1)} %param.19) | copy-start | bytes 772
  10.6 34.6 %copy-start.10 = (bf16[128]{0:T(256)(128)(2,1)S(1)}, bf16[128]{0:T(256)(128)(2,1)}, u32[]{:S(2)}) copy-start(bf16[128]{0:T(256)(128)(2,1)} %param.20) | copy-start | bytes 772
  10.6 34.7 %copy-start.8 = (s32[8]{0:T(128)S(1)}, s32[8]{0:T(128)}, u32[]{:S(2)}) copy-start(s32[8]{0:T(128)} %param.25) | copy-start | bytes 100
  10.6 34.7 %copy-start.1 = (s32[8,64]{1,0:T(8,128)S(1)}, s32[8,64]{1,0:T(8,128)}, u32[]{:S(2)}) copy-start(s32[8,64]{1,0:T(8,128)} %param.24) | copy-start | bytes 6148
  10.6 35.4 %copy-start.7 = (bf16[1024]{0:T(1024)(128)(2,1)S(1)}, bf16[1024]{0:T(1024)(128)(2,1)}, u32[]{:S(2)}) copy-start(bf16[1024]{0:T(1024)(128)(2,1)} %param.18) | copy-start | bytes 6148
  10.6 151.3 %copy-start.3 = (bf16[64,16,8,128]{3,2,1,0:T(8,128)(2,1)S(1)}, bf16[64,16,8,128]{3,2,1,0:T(8,128)(2,1)}, u32[]{:S(2)}) copy-start(bf16[64,16,8,128]{3,2,1,0:T(8,128)(2,1)} %param.23) | copy-start | bytes 6291460
  45.1 257.9 %reduce-scatter.5.cloned.1.call-start = ((), (), s32[]{:S(2)}) async-start(), calls=%async_computation.4 | async-start | bytes 294912 | tf_op jit(solution)/shard_map/reduce_scatter | solution.py:12
  207.4 25.3 %copy-start.2 = (bf16[64,16,8,128]{3,2,1,0:T(8,128)(2,1)}, bf16[64,16,8,128]{3,2,1,0:T(8,128)(2,1)S(1)}, u32[]{:S(2)}) copy-start(bf16[64,16,8,128]{3,2,1,0:T(8,128)(2,1)S(1)} %get-tuple-element.223) | copy-start | bytes 6291460
Sparse Core Ops, SparseCore 0:
  45.2 20.5 reduce-scatter.2
  242.0 60.9 reduce-scatter.4
where the time goes:
time: 312 us; the launch traced here: 311 us
  blocking collectives  145 us (46%)
  waiting for transfers between devices  80.5 us (26%)
  local copies, waits for them, and re-layouts  43.3 us (14%)
  other arithmetic  17 us (5%)
  between operations  14.3 us (5%)
  matrix products  10.4 us (3%)
    reduce_scatter x2, waiting for transfers between devices, summed_rows(): lax.psum_scatter(portion(jnp.int32(0), count), axis, scatter_dimension=0,...  80.5 us
    all_gather x1, blocking collectives, local(): columns = lax.all_gather(tokens, 'tp', axis=1, tiled=True)  32.5 us
    all_gather x1, blocking collectives, local(): lax.all_gather(local_query.reshape(seq_rows, query_cols), 'tp', axis=1, t...  30.5 us
    all_gather x1, blocking collectives, local(): lax.all_gather(value_lin, 'tp', axis=1, tiled=True)  30.5 us
    all_gather x1, blocking collectives, local(): lax.all_gather(key_lin, 'tp', axis=1, tiled=True)  30.4 us
    gather x8, local copies, waits for them, and re-layouts, attend(): key_rows = key_out[slot_ids].reshape(local_span, kv_heads, head_width)  17.5 us
    all_to_all x1, blocking collectives, local(): lax.all_to_all(packed, 'tp', split_axis=2, concat_axis=0, tiled=True)  16 us
  transfers between devices with their start and end apart: 2, of which 2 were waited for; matrix products, arithmetic and copies ran while one was open for 0% of the time, Pallas kernels for 0%

commit v1 on v0

v1 whole, which is shorter than its diff:
```python
import functools

import jax
import jax.numpy as jnp
from jax import lax
from jax.experimental import pallas as pl
from jax.experimental.pallas import tpu as pltpu
from jax.sharding import PartitionSpec as P

rope_theta = 1000000.0
mask_value = -1e30
MESH = pl.DeviceIdType.MESH
f32 = jnp.float32
bf16 = jnp.bfloat16


def lane_round(width):
    return -(-width // 128) * 128


def greet(tp, dp, me_tp, me_dp):
    barrier = pltpu.get_barrier_semaphore()
    for k in range(1, tp):
        pl.semaphore_signal(
            barrier, inc=1, device_id={"tp": lax.rem(me_tp + k, tp)}, device_id_type=MESH
        )
    for k in range(1, dp):
        pl.semaphore_signal(
            barrier, inc=1, device_id={"dp": lax.rem(me_dp + k, dp)}, device_id_type=MESH
        )
    pl.semaphore_wait(barrier, tp - 1 + dp - 1)


def remote(src, dst, send, recv, axis, peer):
    return pltpu.make_async_remote_copy(
        src_ref=src, dst_ref=dst, send_sem=send, recv_sem=recv,
        device_id={axis: peer}, device_id_type=MESH,
    )


def project_kernel(
    dims,
    tok_ref, wq_hbm, wk_hbm, wv_hbm, bq_ref, bk_ref, bv_ref, cs_ref,
    q_out, k_out, v_out,
    wq, wk, wv, tok, part, got, qsend, qgot, kvsend, kvgot,
    wsem, ts, tr, ps, pr, qs, qr, ks, kr,
):
    tp, dp, seq, head, lh, qcols, kcols, kpad = dims
    me, mdp = lax.axis_index("tp"), lax.axis_index("dp")
    width = tok_ref.shape[1]
    order = [lax.rem(me + k, tp) for k in range(tp)]
    wcopies = []
    for k in range(tp):
        t = lax.rem(me + tp - k, tp)
        rows = pl.ds(pl.multiple_of(t * width, width), width)
        c = pltpu.make_async_copy(wq_hbm.at[rows, :], wq.at[rows, :], wsem.at[k])
        c.start()
        wcopies.append(c)
        if k == 0:
            ck = pltpu.make_async_copy(wk_hbm, wk, wsem.at[tp])
            ck.start()
            cv = pltpu.make_async_copy(wv_hbm, wv, wsem.at[tp + 1])
            cv.start()
    greet(tp, dp, me, mdp)
    sends = []
    for k in range(1, tp):
        c = remote(tok_ref, tok.at[k], ts.at[k], tr.at[k], "tp", order[k])
        c.start()
        sends.append(c)
    accq = acck = accv = None
    for k in range(tp):
        t = lax.rem(me + tp - k, tp)
        rows = pl.ds(pl.multiple_of(t * width, width), width)
        wcopies[k].wait()
        if k == 0:
            ck.wait()
            cv.wait()
            block = tok_ref[...]
        else:
            sends[k - 1].wait_recv()
            block = tok[k]
        dq = jnp.dot(block, wq[rows, :], preferred_element_type=f32)
        dk = jnp.dot(block, wk[rows, :], preferred_element_type=f32)
        dv = jnp.dot(block, wv[rows, :], preferred_element_type=f32)
        if k == 0:
            accq, acck, accv = dq, dk, dv
        else:
            accq, acck, accv = accq + dq, acck + dk, accv + dv
    for d in range(dp):
        rs = slice(d * seq, (d + 1) * seq)
        part[d, :, 0:qcols] = accq[rs]
        part[d, :, qcols : qcols + kcols] = acck[rs]
        part[d, :, qcols + kpad : qcols + kpad + kcols] = accv[rs]
    psends = []
    for k in range(1, dp):
        d = lax.rem(mdp + k, dp)
        c = remote(part.at[d], got.at[k], ps.at[k], pr.at[k], "dp", d)
        c.start()
        psends.append(c)
    for c in psends:
        c.wait_recv()
    total = part[mdp]
    for k in range(1, dp):
        total = total + got[k]
    cosine, sine = cs_ref[0], cs_ref[1]
    klin = total[:, qcols : qcols + kcols] + bk_ref[...].astype(f32)
    vlin = total[:, qcols + kpad : qcols + kpad + kcols] + bv_ref[...].astype(f32)
    kvsend[0] = klin
    kvsend[1] = vlin
    for h in range(lh):
        hs = slice(h * head, (h + 1) * head)
        u = total[:, hs] + bq_ref[:, hs].astype(f32)
        r = u * cosine + pltpu.roll(u, head // 2, 1) * sine
        qsend[h * seq : (h + 1) * seq, :] = r.astype(bf16)
    qsends = []
    for k in range(1, tp):
        c = remote(qsend, qgot.at[k], qs.at[k], qr.at[k], "tp", order[k])
        c.start()
        c2 = remote(kvsend, kvgot.at[k], ks.at[k], kr.at[k], "tp", order[k])
        c2.start()
        qsends.append((c, c2))
    rows_dev = lh * seq

    def place(t, qv, kv, vv):
        q_out[t] = qv.astype(f32)
        k_out[t] = kv
        v_out[t] = vv

    place(me, qsend[...], klin, vlin)
    for k in range(1, tp):
        c, c2 = qsends[k - 1]
        c.wait_recv()
        c2.wait_recv()
        place(lax.rem(me + tp - k, tp), qgot[k], kvgot[k, 0], kvgot[k, 1])
    for c in sends + psends:
        c.wait_send()
    for c, c2 in qsends:
        c.wait_send()
        c2.wait_send()


def attend_kernel(
    dims,
    q_ref, kn_ref, vn_ref, cs_ref, table, lengths, kp_hbm, vp_hbm,
    ko_hbm, vo_hbm, o_out, st_out,
    kbuf, vbuf, krot, oscr, mscr, lscr, insem, outsem,
):
    tp, seq, heads, kvh, head, page, slots, pages, parts = dims
    me = lax.axis_index("tp")
    prow = page * kvh
    total_rows = slots * prow
    cut = total_rows // parts
    loads = []
    for i in range(parts):
        r = pl.ds(i * cut, cut)
        a = pltpu.make_async_copy(kp_hbm.at[r, :], kbuf.at[r, :], insem.at[0, i])
        a.start()
        loads.append(a)
    vloads = []
    for i in range(parts):
        r = pl.ds(i * cut, cut)
        a = pltpu.make_async_copy(vp_hbm.at[r, :], vbuf.at[r, :], insem.at[1, i])
        a.start()
        vloads.append(a)
    cosine, sine = cs_ref[0], cs_ref[1]
    for g in range(kvh):
        rs = slice(g * seq, (g + 1) * seq)
        u = kn_ref[rs, :]
        krot[rs, :] = u * cosine + pltpu.roll(u, head // 2, 1) * sine
    rowid = lax.broadcasted_iota(jnp.int32, (2 * kvh, head), 0) // kvh

    def patch(buf, src):
        for b in range(seq):
            length = lengths[b]
            where = length // page
            off = lax.rem(length, page)
            slot = lax.rem(table[b, where], slots)

            @pl.when(lax.rem(where, tp) == me)
            def _():
                base = pl.multiple_of(slot * prow + (off // 2) * (2 * kvh), 2 * kvh)
                fresh = src[pl.ds(b, kvh, stride=seq), :]
                fresh = jnp.concatenate([fresh, fresh], axis=0)
                old = buf[pl.ds(base, 2 * kvh), :].astype(f32)
                buf[pl.ds(base, 2 * kvh), :] = jnp.where(
                    rowid == lax.rem(off, 2), fresh, old
                ).astype(bf16)

    for a in loads:
        a.wait()
    patch(kbuf, krot)
    for a in vloads:
        a.wait()
    patch(vbuf, vn_ref)
    stores = []
    for i, (buf, out) in enumerate(((kbuf, ko_hbm), (vbuf, vo_hbm))):
        a = pltpu.make_async_copy(buf, out, outsem.at[i])
        a.start()
        stores.append(a)
    lane = lax.broadcasted_iota(jnp.int32, (heads, prow), 1)
    hrow = lax.broadcasted_iota(jnp.int32, (heads, prow), 0)
    same = lax.rem(lane, kvh) == hrow // (heads // kvh)
    step = lane // kvh
    scale = head ** (-0.5)
    for b in range(seq):
        length = lengths[b]
        qb = q_ref[pl.ds(b, heads, stride=seq), :].astype(bf16)
        scores, rows = [], []
        for j in range(pages):
            slot = lax.rem(table[b, j * tp + me], slots)
            r = pl.ds(pl.multiple_of(slot * prow, prow), prow)
            rows.append(r)
            s = lax.dot_general(
                qb, kbuf[r, :], (((1,), (1,)), ((), ())), preferred_element_type=f32
            )
            first = (j * tp + me) * page
            scores.append(jnp.where(same & (step <= length - first), s * scale, mask_value))
        peak = functools.reduce(jnp.maximum, scores)
        peak = jnp.max(peak, axis=1, keepdims=True)
        acc = None
        tot = None
        for j in range(pages):
            p = jnp.exp(scores[j] - peak).astype(bf16)
            d = jnp.dot(p, vbuf[rows[j], :], preferred_element_type=f32)
            acc = d if acc is None else acc + d
            pf = p.astype(f32)
            tot = pf if tot is None else tot + pf
        tot = jnp.sum(tot, axis=1, keepdims=True)
        dst = pl.ds(b, heads, stride=seq)
        oscr[dst, :] = acc
        mscr[dst, :] = jnp.broadcast_to(peak, (heads, head))
        lscr[dst, :] = jnp.broadcast_to(tot, (heads, head))
    block = heads // tp * seq
    row = lax.broadcasted_iota(jnp.int32, (block, head), 0)
    col = lax.broadcasted_iota(jnp.int32, (block, head), 1)
    for t in range(tp):
        r = slice(t * block, (t + 1) * block)
        o_out[t] = oscr[r, :].astype(bf16)
        line = jnp.where(col == row, mscr[r, :], 0.0)
        line = line + jnp.where(col == row + block, lscr[r, :], 0.0)
        line = jnp.sum(line, axis=0, keepdims=True)
        st_out[t] = jnp.broadcast_to(line, (8, head))
    for a in stores:
        a.wait()


def mix_kernel(
    dims,
    o_ref, st_ref, w_hbm, out_ref,
    w, og, sg, att, attg, psend, pgot,
    wsem, os, orr, ss, sr, as_, ar, ps, pr,
):
    tp, dp, seq, head, lh, width = dims
    me, mdp = lax.axis_index("tp"), lax.axis_index("dp")
    block = lh * seq
    wc = pltpu.make_async_copy(w_hbm, w, wsem.at[0])
    wc.start()
    greet(tp, dp, me, mdp)
    sends = []
    for k in range(1, tp):
        t = lax.rem(me + k, tp)
        c2 = remote(st_ref.at[t], sg.at[k], ss.at[k], sr.at[k], "tp", t)
        c2.start()
        c = remote(o_ref.at[t], og.at[k], os.at[k], orr.at[k], "tp", t)
        c.start()
        sends.append((c, c2))
    row = lax.broadcasted_iota(jnp.int32, (block, head), 0)
    col = lax.broadcasted_iota(jnp.int32, (block, head), 1)

    def column(line, shift):
        return jnp.sum(jnp.where(col == row + shift, line, 0.0), axis=1, keepdims=True)

    peaks, totals = [], []
    for k in range(tp):
        if k:
            sends[k - 1][1].wait_recv()
            line = sg[k, 0:1, :]
        else:
            line = st_ref[me, 0:1, :]
        peaks.append(column(line, 0))
        totals.append(column(line, block))
    highest = functools.reduce(jnp.maximum, peaks)
    acc = tot = None
    for k in range(tp):
        if k:
            sends[k - 1][0].wait_recv()
            o = og[k]
        else:
            o = o_ref[me]
        fac = jnp.exp(peaks[k] - highest)
        a = o.astype(f32) * fac
        l = totals[k] * fac
        acc = a if acc is None else acc + a
        tot = l if tot is None else tot + l
    res = acc / tot
    for h in range(lh):
        att[:, h * head : (h + 1) * head] = res[h * seq : (h + 1) * seq, :].astype(bf16)
    asends = []
    for k in range(1, dp):
        d = lax.rem(mdp + k, dp)
        c = remote(att, attg.at[mdp], as_.at[k], ar.at[k], "dp", d)
        c.start()
        asends.append(c)
    attg[mdp] = att[...]
    for c in asends:
        c.wait_recv()
    rows = jnp.concatenate([attg[d].astype(f32) for d in range(dp)], axis=0).astype(bf16)
    wc.wait()
    aligned = width % 128 == 0
    if not aligned:
        for t in range(tp):
            ws = w[:, t * width : (t + 1) * width]
            psend[t] = jnp.dot(rows, ws, preferred_element_type=f32).astype(bf16)

    def product(t):
        ws = w[:, pl.ds(pl.multiple_of(t * width, width), width)]
        return jnp.dot(rows, ws, preferred_element_type=f32)

    psends = []
    for k in range(1, tp):
        t = lax.rem(me + k, tp)
        if aligned:
            psend[t] = product(t).astype(bf16)
        c = remote(psend.at[t], pgot.at[k], ps.at[k], pr.at[k], "tp", t)
        c.start()
        psends.append(c)
    total = product(me) if aligned else psend[me].astype(f32)
    for k in range(1, tp):
        psends[k - 1].wait_recv()
        total = total + pgot[k].astype(f32)
    out_ref[...] = total.astype(bf16)
    for c, c2 in sends:
        c.wait_send()
        c2.wait_send()
    for c in asends + psends:
        c.wait_send()


def local(
    tokens, query_weight, key_weight, value_weight, query_bias, key_bias, value_bias,
    out_weight, key_pool, value_pool, page_table, lengths,
):
    tp, dp = lax.axis_size("tp"), lax.axis_size("dp")
    seq = page_table.shape[0]
    slots, page, kvh, head = key_pool.shape
    depth, qcols = query_weight.shape
    kcols = key_weight.shape[1]
    kpad = lane_round(kcols)
    lh = qcols // head
    heads = lh * tp
    batch, width = tokens.shape
    pages = page_table.shape[1] // tp
    block = lh * seq
    half = head // 2
    frequency = rope_theta ** (-(jnp.arange(half, dtype=f32) * 2.0 / head))
    angles = lengths.astype(f32)[:, None] * frequency[None, :]
    cosine, sine = jnp.cos(angles), jnp.sin(angles)
    cs = jnp.stack(
        [jnp.concatenate([cosine, cosine], 1), jnp.concatenate([-sine, sine], 1)]
    )
    vm = pl.BlockSpec(memory_space=pltpu.VMEM)
    hbm = pl.BlockSpec(memory_space=pltpu.HBM)
    sm = pl.BlockSpec(memory_space=pltpu.SMEM)
    dma = pltpu.SemaphoreType.DMA
    q, kn, vn = pl.pallas_call(
        functools.partial(project_kernel, (tp, dp, seq, head, lh, qcols, kcols, kpad)),
        out_shape=(
            jax.ShapeDtypeStruct((tp, block, head), f32),
            jax.ShapeDtypeStruct((tp, seq, kcols), f32),
            jax.ShapeDtypeStruct((tp, seq, kcols), f32),
        ),
        in_specs=[vm, hbm, hbm, hbm, vm, vm, vm, vm],
        out_specs=(vm, vm, vm),
        scratch_shapes=[
            pltpu.VMEM((depth, qcols), bf16),
            pltpu.VMEM((depth, kcols), bf16),
            pltpu.VMEM((depth, kcols), bf16),
            pltpu.VMEM((tp, batch, width), bf16),
            pltpu.VMEM((dp, seq, qcols + 2 * kpad), f32),
            pltpu.VMEM((dp, seq, qcols + 2 * kpad), f32),
            pltpu.VMEM((block, head), bf16),
            pltpu.VMEM((tp, block, head), bf16),
            pltpu.VMEM((2, seq, kcols), f32),
            pltpu.VMEM((tp, 2, seq, kcols), f32),
            dma((tp + 2,)),
            dma((tp,)), dma((tp,)), dma((dp,)), dma((dp,)),
            dma((tp,)), dma((tp,)), dma((tp,)), dma((tp,)),
        ],
        compiler_params=pltpu.CompilerParams(
            collective_id=0, has_side_effects=True, vmem_limit_bytes=24 * 2**20
        ),
        name="project",
    )(
        tokens, query_weight, key_weight, value_weight,
        query_bias[None], key_bias[None], value_bias[None], cs,
    )
    if kcols != head:
        kn = kn.transpose(1, 0, 2).reshape(seq, kvh, head).transpose(1, 0, 2)
        vn = vn.transpose(1, 0, 2).reshape(seq, kvh, head).transpose(1, 0, 2)
    rows = slots * page * kvh
    parts = 4
    ko, vo, o, st = pl.pallas_call(
        functools.partial(
            attend_kernel, (tp, seq, heads, kvh, head, page, slots, pages, parts)
        ),
        out_shape=(
            jax.ShapeDtypeStruct((rows, head), bf16),
            jax.ShapeDtypeStruct((rows, head), bf16),
            jax.ShapeDtypeStruct((tp, block, head), bf16),
            jax.ShapeDtypeStruct((tp, 8, head), f32),
        ),
        in_specs=[vm, vm, vm, vm, sm, sm, hbm, hbm],
        out_specs=(hbm, hbm, vm, vm),
        scratch_shapes=[
            pltpu.VMEM((rows, head), bf16),
            pltpu.VMEM((rows, head), bf16),
            pltpu.VMEM((kvh * seq, head), f32),
            pltpu.VMEM((heads * seq, head), f32),
            pltpu.VMEM((heads * seq, head), f32),
            pltpu.VMEM((heads * seq, head), f32),
            dma((2, parts)),
            dma((2,)),
        ],
        compiler_params=pltpu.CompilerParams(vmem_limit_bytes=24 * 2**20),
        name="attend",
    )(
        q.reshape(heads * seq, head), kn.reshape(kvh * seq, head), vn.reshape(kvh * seq, head),
        cs, page_table, lengths,
        key_pool.reshape(rows, head), value_pool.reshape(rows, head),
    )
    out_width = out_weight.shape[1] // tp
    mixed = pl.pallas_call(
        functools.partial(mix_kernel, (tp, dp, seq, head, lh, out_width)),
        out_shape=jax.ShapeDtypeStruct((batch, out_width), bf16),
        in_specs=[vm, vm, hbm],
        out_specs=vm,
        scratch_shapes=[
            pltpu.VMEM(out_weight.shape, bf16),
            pltpu.VMEM((tp, block, head), bf16),
            pltpu.VMEM((tp, 8, head), f32),
            pltpu.VMEM((seq, qcols), bf16),
            pltpu.VMEM((dp, seq, qcols), bf16),
            pltpu.VMEM((tp, batch, out_width), bf16),
            pltpu.VMEM((tp, batch, out_width), bf16),
            dma((1,)),
            dma((tp,)), dma((tp,)), dma((tp,)), dma((tp,)),
            dma((dp,)), dma((dp,)), dma((tp,)), dma((tp,)),
        ],
        compiler_params=pltpu.CompilerParams(
            collective_id=1, has_side_effects=True, vmem_limit_bytes=24 * 2**20
        ),
        name="mix",
    )(o, st, out_weight)
    return mixed, ko.reshape(key_pool.shape), vo.reshape(value_pool.shape)


def solution(mesh):
    in_specs = (
        P(None, ("dp", "tp")),
        P("dp", "tp"),
        P("dp", "tp"),
        P("dp", "tp"),
        P("tp"),
        P("tp"),
        P("tp"),
        P("tp", "dp"),
        P(("dp", "tp"), None, None, None),
        P(("dp", "tp"), None, None, None),
        P("dp", None),
        P("dp"),
    )
    out_specs = (
        P(None, ("dp", "tp")),
        P(("dp", "tp"), None, None, None),
        P(("dp", "tp"), None, None, None),
    )
    return jax.shard_map(local, mesh=mesh, in_specs=in_specs, out_specs=out_specs, check_vma=False)
```

time: 312 us -> 55.3 us (0.18)
  blocking collectives: 145 us -> 0 us
  waiting for transfers between devices: 80.5 us -> 0 us
  Pallas kernels: 0 us -> 45.7 us
  local copies, waits for them, and re-layouts: 43.3 us -> 7.62 us
  other arithmetic: 17 us -> 0.86 us
  between operations: 14.3 us -> 0.71 us
  matrix products: 10.4 us -> 0 us
    all_gather x5 -> x0, blocking collectives: 129 us -> none  [the longest x1 32.5 us: local(): columns = lax.all_gather(tokens, 'tp', axis=1, tiled=True)]
    reduce_scatter x2 -> x0, waiting for transfers between devices: 80.5 us -> none  [summed_rows(): lax.psum_scatter(portion(jnp.int32(0), count), axis, scatter_dimension=0,...]
    pallas_call x0 -> x3, Pallas kernels: none -> 45.7 us  [the longest x1 21.3 us: local(): pl.pallas_call(functools.partial(project_kernel, (tp, dp, seq, head, lh,...]
    gather x17 -> x0, local copies, waits for them, and re-layouts: 23 us -> none  [the longest x8 17.5 us: attend(): key_rows = key_out[slot_ids].reshape(local_span, kv_heads, head_width)]
    all_to_all x1 -> x0, blocking collectives: 16 us -> none  [local(): lax.all_to_all(packed, 'tp', split_axis=2, concat_axis=0, tiled=True)]
    dot_general x20 -> x0, matrix products: 10.4 us -> none  [the longest x1 3.71 us: mix(): lax.dot_general(weight_block, batch_heads, (((0,), (1,)), ((), ())), pref...]
    dynamic_slice x17 -> x0, local copies, waits for them, and re-layouts: 5.88 us -> none  [the longest x16 5.6 us: local(): lax.map(attend, (query_rows, local_ids, lengths))]
    le x8 -> x0, other arithmetic: 5.74 us -> none  [attend(): scores = jnp.where(positions[None, None, :] <= length, scores, mask_value)]
  transfers between devices with their start and end apart: 2 -> 0, of which waited for: 2 -> 0; matrix products, arithmetic and copies ran while one was open for 0% -> 0% of each run, Pallas kernels for 0% -> 0%
where the time goes in v1:
time: 55.3 us; the launch traced here: 54.9 us
  Pallas kernels  45.7 us (83%)
  local copies, waits for them, and re-layouts  7.62 us (14%)
  other arithmetic  0.86 us (2%)
  between operations  0.71 us (1%)
    pallas_call x1, Pallas kernels, local(): pl.pallas_call(functools.partial(project_kernel, (tp, dp, seq, head, lh,...  21.3 us
    pallas_call x1, Pallas kernels, local(): pl.pallas_call(functools.partial(mix_kernel, (tp, dp, seq, head, lh, out_...  18 us
    unnamed x23, local copies, waits for them, and re-layouts  6.93 us
    pallas_call x1, Pallas kernels, local(): pl.pallas_call(functools.partial(attend_kernel, (tp, seq, heads, kvh, hea...  6.48 us

profile of v1, /device:TPU:0, one launch (start us, length us, event | category | flops | bytes accessed | tf_op | source)
XLA Modules:
  0.0 54.9 jit_solution(18096665344543719772)
XLA Ops:
  0.6 0.7 %convert_element_type.3 = f32[8]{0:T(128)S(1)} convert(s32[8]{0:T(128)} %lengths.1) | non-fusion elementwise | flops 8 | bytes 64 | tf_op jit(solution)/shard_map/convert_element_type | solution.py:356
  1.3 0.7 %broadcast_in_dim.11.bq_ref = bf16[1,1024]{1,0:T(2,128)(2,1)S(1)} reshape(bf16[1024]{0:T(1024)(128)(2,1)} %param.16) | data formatting | bytes 4096 | tf_op jit(solution)/shard_map/broadcast_in_dim | solution.py:395
  2.0 0.1 multiply_cosine_fusion
  2.1 0.1 maximum_bitcast_fusion
  2.2 0.0 copy-start
  2.2 2.2 %copy-done = bf16[2048,1024]{1,0:T(8,128)(2,1)S(1)} copy-done((bf16[2048,1024]{1,0:T(8,128)(2,1)S(1)}, bf16[2048,1024]{1,0:T(8,128)(2,1)}, u32[]{:S(2)}) %copy-start) | copy-done | bytes 4194328
  4.4 0.0 copy-start.4
  4.4 1.0 %copy-done.4 = bf16[2048,128]{1,0:T(8,128)(2,1)S(1)} copy-done((bf16[2048,128]{1,0:T(8,128)(2,1)S(1)}, bf16[2048,128]{1,0:T(8,128)(2,1)}, u32[]{:S(2)}) %copy-start.4) | copy-done | bytes 524312
  5.4 0.0 copy-start.5
  5.4 1.0 %copy-done.5 = bf16[2048,128]{1,0:T(8,128)(2,1)S(1)} copy-done((bf16[2048,128]{1,0:T(8,128)(2,1)S(1)}, bf16[2048,128]{1,0:T(8,128)(2,1)}, u32[]{:S(2)}) %copy-start.5) | copy-done | bytes 524312
  6.5 0.0 copy-start.6
  6.5 0.7 %copy-done.6 = bf16[32,256]{1,0:T(8,128)(2,1)S(1)} copy-done((bf16[32,256]{1,0:T(8,128)(2,1)S(1)}, bf16[32,256]{1,0:T(8,128)(2,1)}, u32[]{:S(2)}) %copy-start.6) | copy-done | bytes 16408
  7.2 0.7 %copy-done.8 = bf16[128]{0:T(256)(128)(2,1)S(1)} copy-done((bf16[128]{0:T(256)(128)(2,1)S(1)}, bf16[128]{0:T(256)(128)(2,1)}, u32[]{:S(2)}) %copy-start.8) | copy-done | bytes 280
  7.8 0.7 %copy-done.9 = bf16[128]{0:T(256)(128)(2,1)S(1)} copy-done((bf16[128]{0:T(256)(128)(2,1)S(1)}, bf16[128]{0:T(256)(128)(2,1)}, u32[]{:S(2)}) %copy-start.9) | copy-done | bytes 280
  8.5 21.3 %project.1 = (f32[8,64,128]{2,1,0:T(8,128)S(1)}, f32[8,8,128]{2,1,0:T(8,128)S(1)}, f32[8,8,128]{2,1,0:T(8,128)S(1)}) custom-call(bf16[32,256]{1,0:T(8,128)(2,1)S(1)} %copy-done.6, bf16[2048,1024]{1,0:T(8,128)(2,1)S(1)} %copy-done, bf16[2048,128]{1,0:T(8,128)(2,1)S(1)} %copy-done.4, bf16[2048,128]{1,0:T(8,128)(2,1)S(1)} %copy-done.5, ...), custom_call_target="tpu_custom_call" | custom-call | tf_op jit(solution)/shard_map/project/pallas_call | solution.py:365
  29.8 0.0 copy-done.2
  29.8 0.0 copy-done.3
  29.8 0.0 copy-done.7
  29.8 0.0 copy-done.10
  29.8 0.0 copy-start.1
  29.9 6.5 %attend.1 = (bf16[8192,128]{1,0:T(8,128)(2,1)}, bf16[8192,128]{1,0:T(8,128)(2,1)}, bf16[8,64,128]{2,1,0:T(8,128)(2,1)S(1)}, f32[8,8,128]{2,1,0:T(8,128)S(1)}) custom-call(f32[512,128]{1,0:T(8,128)S(1)} %bitcast.15, f32[64,128]{1,0:T(8,128)S(1)} %bitcast.16, f32[64,128]{1,0:T(8,128)S(1)} %bitcast.17, f32[2,8,128]{2,1,0:T(8,128)S(1)} %pad_maximum_fusion.cs_ref, ...), custom_call_target="tpu_custom_call" | custom-call | tf_op jit(solution)/shard_map/attend/pallas_call | solution.py:402
  36.3 0.0 copy-done.1
  36.3 18.0 %mix.1 = bf16[32,256]{1,0:T(8,128)(2,1)S(1)} custom-call(bf16[8,64,128]{2,1,0:T(8,128)(2,1)S(1)} %get-tuple-element.13.o_ref, f32[8,8,128]{2,1,0:T(8,128)S(1)} %get-tuple-element.14.st_ref, bf16[1024,2048]{1,0:T(8,128)(2,1)S(1)} %copy-done.1), custom_call_target="tpu_custom_call" | custom-call | tf_op jit(solution)/shard_map/mix/pallas_call | solution.py:432
  54.3 0.6 %copy.16 = bf16[32,256]{1,0:T(8,128)(2,1)} copy(bf16[32,256]{1,0:T(8,128)(2,1)S(1)} %mix.1) | data formatting | bytes 32768
  (8 shorter events, 0.0 us)
Async XLA Ops:
  2.2 2.2 %copy-start = (bf16[2048,1024]{1,0:T(8,128)(2,1)S(1)}, bf16[2048,1024]{1,0:T(8,128)(2,1)}, u32[]{:S(2)}) copy-start(bf16[2048,1024]{1,0:T(8,128)(2,1)} %wq_hbm.1) | copy-start | bytes 12582916
  4.4 1.0 %copy-start.4 = (bf16[2048,128]{1,0:T(8,128)(2,1)S(1)}, bf16[2048,128]{1,0:T(8,128)(2,1)}, u32[]{:S(2)}) copy-start(bf16[2048,128]{1,0:T(8,128)(2,1)} %wk_hbm.1) | copy-start | bytes 1572868
  5.4 1.0 %copy-start.5 = (bf16[2048,128]{1,0:T(8,128)(2,1)S(1)}, bf16[2048,128]{1,0:T(8,128)(2,1)}, u32[]{:S(2)}) copy-start(bf16[2048,128]{1,0:T(8,128)(2,1)} %wv_hbm.1) | copy-start | bytes 1572868
  6.5 0.7 %copy-start.6 = (bf16[32,256]{1,0:T(8,128)(2,1)S(1)}, bf16[32,256]{1,0:T(8,128)(2,1)}, u32[]{:S(2)}) copy-start(bf16[32,256]{1,0:T(8,128)(2,1)} %tok_ref.1) | copy-start | bytes 49156
  7.2 0.7 %copy-start.8 = (bf16[128]{0:T(256)(128)(2,1)S(1)}, bf16[128]{0:T(256)(128)(2,1)}, u32[]{:S(2)}) copy-start(bf16[128]{0:T(256)(128)(2,1)} %param.17) | copy-start | bytes 772
  7.8 0.7 %copy-start.9 = (bf16[128]{0:T(256)(128)(2,1)S(1)}, bf16[128]{0:T(256)(128)(2,1)}, u32[]{:S(2)}) copy-start(bf16[128]{0:T(256)(128)(2,1)} %param.18) | copy-start | bytes 772
  8.5 21.3 %copy-start.2 = (bf16[64,16,8,128]{3,2,1,0:T(8,128)(2,1)S(1)}, bf16[64,16,8,128]{3,2,1,0:T(8,128)(2,1)}, u32[]{:S(2)}) copy-start(bf16[64,16,8,128]{3,2,1,0:T(8,128)(2,1)} %param.20) | copy-start | bytes 6291460
  8.5 21.3 %copy-start.3 = (bf16[64,16,8,128]{3,2,1,0:T(8,128)(2,1)S(1)}, bf16[64,16,8,128]{3,2,1,0:T(8,128)(2,1)}, u32[]{:S(2)}) copy-start(bf16[64,16,8,128]{3,2,1,0:T(8,128)(2,1)} %param.21) | copy-start | bytes 6291460
  8.5 21.3 %copy-start.7 = (s32[8,64]{1,0:T(8,128)S(1)}, s32[8,64]{1,0:T(8,128)}, u32[]{:S(2)}) copy-start(s32[8,64]{1,0:T(8,128)} %table.1) | copy-start | bytes 6148
  8.5 21.3 %copy-start.10 = (s32[8]{0:T(128)S(1)}, s32[8]{0:T(128)}, u32[]{:S(2)}) copy-start(s32[8]{0:T(128)} %lengths.1) | copy-start | bytes 100
  29.8 6.5 %copy-start.1 = (bf16[1024,2048]{1,0:T(8,128)(2,1)S(1)}, bf16[1024,2048]{1,0:T(8,128)(2,1)}, u32[]{:S(2)}) copy-start(bf16[1024,2048]{1,0:T(8,128)(2,1)} %w_hbm.1) | copy-start | bytes 12582916

commit v2 on v1

--- a/solution.py
+++ b/solution.py
@@ -387,7 +387,7 @@
             dma((tp,)), dma((tp,)), dma((tp,)), dma((tp,)),
         ],
         compiler_params=pltpu.CompilerParams(
-            collective_id=0, has_side_effects=True, vmem_limit_bytes=24 * 2**20
+            collective_id=0, has_side_effects=True
         ),
         name="project",
     )(
@@ -421,7 +421,6 @@
             dma((2, parts)),
             dma((2,)),
         ],
-        compiler_params=pltpu.CompilerParams(vmem_limit_bytes=24 * 2**20),
         name="attend",
     )(
         q.reshape(heads * seq, head), kn.reshape(kvh * seq, head), vn.reshape(kvh * seq, head),
@@ -447,7 +446,7 @@
             dma((dp,)), dma((dp,)), dma((tp,)), dma((tp,)),
         ],
         compiler_params=pltpu.CompilerParams(
-            collective_id=1, has_side_effects=True, vmem_limit_bytes=24 * 2**20
+            collective_id=1, has_side_effects=True
         ),
         name="mix",
     )(o, st, out_weight)

time: 55.3 us -> 53.9 us (0.975)
  local copies, waits for them, and re-layouts: 7.62 us -> 2.61 us
  Pallas kernels: 45.7 us -> 48.9 us
  other arithmetic: 0.86 us -> 1.46 us
    unnamed x23 -> x1, local copies, waits for them, and re-layouts: 6.93 us -> 1.32 us
    pallas_call x1, Pallas kernels: 18 us -> 19.2 us  [local(): pl.pallas_call(functools.partial(mix_kernel, (tp, dp, seq, head, lh, out_...]
    pallas_call x1, Pallas kernels: 21.3 us -> 22.4 us  [local(): pl.pallas_call(functools.partial(project_kernel, (tp, dp, seq, head, lh,...]
    pallas_call x1, Pallas kernels: 6.48 us -> 7.34 us  [local(): pl.pallas_call(functools.partial(attend_kernel, (tp, seq, heads, kvh, hea...]
    another operation x2, other arithmetic: 0.08 us -> 0.68 us  [local(): jnp.stack([jnp.concatenate([cosine, cosine], 1), jnp.concatenate([-sine,...]
    broadcast_in_dim x1, local copies, waits for them, and re-layouts: 0.69 us -> 1.28 us  [local(): query_bias[None]]
where the time goes in v2:
time: 53.9 us; the launch traced here: 53.6 us
  Pallas kernels  48.9 us (91%)
  local copies, waits for them, and re-layouts  2.61 us (5%)
  other arithmetic  1.46 us (3%)
  between operations  0.66 us (1%)
    pallas_call x1, Pallas kernels, local(): pl.pallas_call(functools.partial(project_kernel, (tp, dp, seq, head, lh,...  22.4 us
    pallas_call x1, Pallas kernels, local(): pl.pallas_call(functools.partial(mix_kernel, (tp, dp, seq, head, lh, out_...  19.2 us
    pallas_call x1, Pallas kernels, local(): pl.pallas_call(functools.partial(attend_kernel, (tp, seq, heads, kvh, hea...  7.34 us
    unnamed x1, local copies, waits for them, and re-layouts  1.32 us
    broadcast_in_dim x1, local copies, waits for them, and re-layouts, local(): query_bias[None]  1.28 us

profile of v2, /device:TPU:0, one launch (start us, length us, event | category | flops | bytes accessed | tf_op | source)
XLA Modules:
  0.0 53.6 jit_solution(4846917528500353786)
XLA Ops:
  0.6 0.7 %convert_element_type.3 = f32[8]{0:T(128)S(1)} convert(s32[8]{0:T(128)} %lengths.1) | non-fusion elementwise | flops 8 | bytes 64 | tf_op jit(solution)/shard_map/convert_element_type | solution.py:356
  1.3 1.3 %broadcast_in_dim.11.bq_ref = bf16[1,1024]{1,0:T(2,128)(2,1)} reshape(bf16[1024]{0:T(1024)(128)(2,1)} %param.16) | data formatting | bytes 4096 | tf_op jit(solution)/shard_map/broadcast_in_dim | solution.py:395
  2.6 0.1 multiply_cosine_fusion
  2.7 0.1 maximum_bitcast_fusion
  2.8 0.6 %pad_maximum_fusion.cs_ref = f32[2,8,128]{2,1,0:T(8,128)} fusion(f32[1,8,128]{2,1,0:T(8,128)S(1)} %get-tuple-element.21, f32[1,8,128]{2,1,0:T(8,128)S(1)} %get-tuple-element.20), kind=kLoop, calls=%fused_computation | loop fusion | flops 2048 | bytes 16384 | tf_op jit(solution)/shard_map/stack | solution.py:358
  3.4 22.4 %project.1 = (f32[8,64,128]{2,1,0:T(8,128)}, f32[8,8,128]{2,1,0:T(8,128)}, f32[8,8,128]{2,1,0:T(8,128)}) custom-call(bf16[32,256]{1,0:T(8,128)(2,1)} %tok_ref.1, bf16[2048,1024]{1,0:T(8,128)(2,1)} %wq_hbm.1, bf16[2048,128]{1,0:T(8,128)(2,1)} %wk_hbm.1, bf16[2048,128]{1,0:T(8,128)(2,1)} %wv_hbm.1, bf16[1,1024]{1,0:T(2,128)(2,1)} %broadcast_in_dim.11.bq_ref, ...), custom_call_target="tpu_custom_call" | custom-call | tf_op jit(solution)/shard_map/project/pallas_call | solution.py:365
  25.7 7.3 %attend.1 = (bf16[8192,128]{1,0:T(8,128)(2,1)}, bf16[8192,128]{1,0:T(8,128)(2,1)}, bf16[8,64,128]{2,1,0:T(8,128)(2,1)}, f32[8,8,128]{2,1,0:T(8,128)}) custom-call(f32[512,128]{1,0:T(8,128)} %bitcast.15, f32[64,128]{1,0:T(8,128)} %bitcast.16, f32[64,128]{1,0:T(8,128)} %bitcast.17, f32[2,8,128]{2,1,0:T(8,128)} %pad_maximum_fusion.cs_ref, s32[8,64]{1,0:T(8,128)} %table.1, ...), custom_call_target="tpu_custom_call" | custom-call | tf_op jit(solution)/shard_map/attend/pallas_call | solution.py:402
  33.1 19.2 %mix.1 = bf16[32,256]{1,0:T(8,128)(2,1)} custom-call(bf16[8,64,128]{2,1,0:T(8,128)(2,1)} %get-tuple-element.13.o_ref, f32[8,8,128]{2,1,0:T(8,128)} %get-tuple-element.14.st_ref, bf16[1024,2048]{1,0:T(8,128)(2,1)} %w_hbm.1), custom_call_target="tpu_custom_call" | custom-call | tf_op jit(solution)/shard_map/mix/pallas_call | solution.py:431
  52.3 1.3 %copy.16 = bf16[32,256]{1,0:T(8,128)(2,1)} copy(bf16[32,256]{1,0:T(8,128)(2,1)} %mix.1) | data formatting | bytes 32768
  (1 shorter events, 0.0 us)
